TPU v7x, 256 devices: a whole 4x4x8 slice. The times are simulated.
256 devices in a mesh: ctx: 16 (over z_hi, x, core), exp: 16 (over y, z_lo).
Axes of the slice: x: 4, y: 4, z: 8 (z_hi: 2, z_lo: 4; z = z_hi * 4 + z_lo), core: 2. Of those that a mesh axis runs over, the one named last changes fastest.
Arguments:
- q_nope: bfloat16 [1024, 128, 512], P('ctx', 'exp'), may hold values from -72 to 72
- q_rope: bfloat16 [1024, 8192], P('ctx', 'exp'), may hold values from -6 to 6
- cache_keys: bfloat16 [576, 2048], P(None, 'ctx'), may hold values from -6 to 6
- fresh_keys: bfloat16 [576, 1024], P(None, 'ctx'), may hold values from -6 to 6
- block_order: int32 [32], replicated, may hold values from 0 to 31, each once
- w_uv: bfloat16 [128, 512, 128], P('exp'), may hold values from -0.25 to 0.25
- w_out: bfloat16 [16384, 7168], P('exp', 'ctx'), may hold values from -0.046875 to 0.046875
- residual: bfloat16 [1024, 7168], P(('ctx', 'exp')), may hold values from -6 to 6
- norm_gain: float32 [7168], replicated, may hold values from 0.5 to 1.5
- router_weight: bfloat16 [7168, 16], replicated, may hold values from -0.0625 to 0.0625
- expert_ids: int32 [1024, 8], P(('ctx', 'exp')), may hold values from 0 to 15, all different within a row; in each aligned block of 4 rows (0 to 3, 4 to 7, ...) at most 3 rows name the same one
- w_gate: bfloat16 [16, 7168, 2048], P('exp', None, 'ctx'), may hold values from -0.0625 to 0.0625
- w_up: bfloat16 [16, 7168, 2048], P('exp', None, 'ctx'), may hold values from -0.0625 to 0.0625
- w_down: bfloat16 [16, 2048, 7168], P('exp', 'ctx'), may hold values from -0.125 to 0.125
Outputs:
- layer_out: bfloat16 [1024, 7168], P(('ctx', 'exp'))
Inputs may be any that keep to these rules, and one draw needn't show every extreme that they name: A permutation: block j of the new tokens (32 rows) sits at positions 2048 + block_order[j] * 32 onward. `expert_ids`: each row names 8 different experts; the 4 rows of one device name no expert more than 3 times, and in some aligned block one expert exactly 3 times.
All inputs are finite; a program needn't handle non-finite values.
Results may differ from a plain program's by a relative error of at most 0.012.
Values may be sent and summed in bfloat16 or wider, within the bound.
A program may use at most 128 MiB of HBM per device.

v0:
```python
import math

import jax
import jax.numpy as jnp
from jax import lax
from jax.sharding import PartitionSpec as P

QKD = 192
CAP = 3


ROUTE_SCALE = 2.5
NORM_EPS = 1e-06


def copy_for_each(value, axis):
    copies = jnp.broadcast_to(value, (lax.axis_size(axis), *value.shape))
    return lax.all_to_all(copies, axis, split_axis=0, concat_axis=0, tiled=True)


def in_order(pieces, dim):
    pieces = jnp.moveaxis(pieces, 0, dim)
    shape = pieces.shape
    return pieces.reshape(*shape[:dim], shape[dim] * shape[dim + 1], *shape[dim + 2 :])


def gather_directly(value, axis, dim):
    pieces = copy_for_each(value, axis)
    return in_order(pieces, dim)


def in_blocks(value, dim, length):
    shape = value.shape
    pieces = value.reshape(*shape[:dim], length, shape[dim] // length, *shape[dim + 1 :])
    return jnp.moveaxis(pieces, dim, 0)


def sum_at_owner(value, axis, dim):
    length = lax.axis_size(axis)
    pieces = lax.all_to_all(in_blocks(value, dim, length), axis, 0, 0, tiled=True)
    return jnp.sum(pieces.astype(jnp.float32), axis=0)


def block_position(row_index, block_order, block_rows):
    blocks = row_index // block_rows
    lookup = blocks[:, None] == jnp.arange(block_order.shape[0], dtype=jnp.int32)[None, :]
    leading = jnp.sum(jnp.where(lookup, block_order[None, :], 0), axis=1)
    return leading * block_rows + row_index % block_rows


def attend(query_lat, query_pe, keys, visible):
    row_count, head_count, latent_width = query_lat.shape
    key_count = keys.shape[1]
    pe_width = query_pe.shape[1] // head_count
    first_dot = jnp.dot(
        query_lat.reshape(row_count * head_count, latent_width),
        keys[:latent_width],
        preferred_element_type=jnp.float32,
    )
    second_dot = jnp.dot(
        query_pe.reshape(row_count * head_count, pe_width),
        keys[latent_width:],
        preferred_element_type=jnp.float32,
    )
    scores = ((first_dot + second_dot) * (1.0 / math.sqrt(QKD))).reshape(
        row_count, head_count, key_count
    )
    scores = jnp.where(visible[:, None, :], scores, -jnp.inf)
    row_max = jnp.max(scores, axis=2)
    exponent = jnp.exp(scores - row_max[:, :, None])
    row_sum = jnp.sum(exponent, axis=2)
    weights = exponent.astype(jnp.bfloat16).reshape(row_count * head_count, key_count)
    latent = lax.dot_general(
        weights, keys[:latent_width], (((1,), (1,)), ((), ())), preferred_element_type=jnp.float32
    )
    return (row_max, row_sum, latent.reshape(row_count, head_count, latent_width))


def merge_partial(earlier, latter):
    highest = latter[0]
    earlier_scale = jnp.exp(earlier[0] - highest)
    latter_scale = jnp.exp(latter[0] - highest)
    row_sum = earlier_scale * earlier[1] + latter_scale * latter[1]
    latent = earlier_scale[:, :, None] * earlier[2] + latter_scale[:, :, None] * latter[2]
    return (highest, row_sum, latent)


def body(
    q_nope,
    q_rope,
    cache_keys,
    fresh_keys,
    block_order,
    w_uv,
    w_out,
    residual,
    norm_gain,
    router_weight,
    expert_ids,
    w_gate,
    w_up,
    w_down,
):
    ctx_count = lax.axis_size("ctx")
    exp_count = lax.axis_size("exp")
    ctx_index = lax.axis_index("ctx")
    rows_here, heads_here, latent_width = q_nope.shape
    value_width = w_uv.shape[2]
    cache_len = cache_keys.shape[1]
    key_cols = cache_len + rows_here
    block_rows = rows_here // 2
    keys_here = jnp.concatenate([cache_keys, fresh_keys], axis=1)
    w_uv_wide = w_uv.astype(jnp.float32)
    own_rows = ctx_index * rows_here + jnp.arange(rows_here, dtype=jnp.int32)
    own_pos = block_position(own_rows, block_order, block_rows)
    start_state = (
        jnp.full((rows_here, heads_here), -jnp.inf, jnp.float32),
        jnp.zeros((rows_here, heads_here), jnp.float32),
        jnp.zeros((rows_here, heads_here, latent_width), jnp.float32),
    )
    portion = lax.all_gather(keys_here, "ctx", axis=1, tiled=True)
    columns = jnp.arange(portion.shape[1], dtype=jnp.int32)
    owner_dev = columns // key_cols
    within = columns % key_cols
    fresh_row = owner_dev * rows_here + within - cache_len
    key_pos = jnp.where(within < cache_len, -1, block_position(fresh_row, block_order, block_rows))
    visible = key_pos[None, :] <= own_pos[:, None]
    row_max, row_sum, latent = merge_partial(start_state, attend(q_nope, q_rope, portion, visible))
    normal_lat = latent / row_sum[:, :, None]
    head_wide = jnp.einsum("rhl,hlv->rhv", normal_lat, w_uv_wide, precision=lax.Precision.HIGHEST)
    head_out = head_wide.astype(jnp.bfloat16).reshape(rows_here, heads_here * value_width)
    tok_here, model_width = residual.shape
    col_part = w_out.shape[1]
    head_partial = jnp.dot(
        gather_directly(head_out, "ctx", 0), w_out, preferred_element_type=jnp.float32
    )
    arranged = head_partial.reshape(ctx_count, exp_count, tok_here, col_part)
    head_total = sum_at_owner(arranged.astype(jnp.bfloat16), "exp", 1)
    attention = lax.all_to_all(
        head_total.astype(jnp.bfloat16), "ctx", split_axis=0, concat_axis=3, tiled=True
    ).reshape(tok_here, model_width)
    hidden = residual.astype(jnp.float32) + attention.astype(jnp.float32)
    mean_square = jnp.mean(hidden * hidden, axis=1, keepdims=True)
    normed = (hidden * lax.rsqrt(mean_square + NORM_EPS) * norm_gain).astype(jnp.bfloat16)
    affinity = jax.nn.sigmoid(jnp.dot(normed, router_weight, preferred_element_type=jnp.float32))
    expert_count = router_weight.shape[1]
    onehot = expert_ids[:, :, None] == jnp.arange(expert_count, dtype=jnp.int32)[None, None, :]
    chosen = jnp.sum(jnp.where(onehot, affinity[:, None, :], 0.0), axis=2)
    route = ROUTE_SCALE * chosen / jnp.sum(chosen, axis=1, keepdims=True)
    mixing = jnp.sum(jnp.where(onehot, route[:, :, None], 0.0), axis=1)
    picked = jnp.sum(onehot.astype(jnp.int32), axis=1)
    slot_index = jnp.cumsum(picked, axis=0) - picked
    slot_hot = (slot_index[:, :, None] == jnp.arange(CAP, dtype=jnp.int32)[None, None, :]) & (
        picked[:, :, None] > 0
    )
    dispatch_map = (
        jnp.transpose(slot_hot, (1, 2, 0))
        .reshape(expert_count * CAP, tok_here)
        .astype(jnp.bfloat16)
    )
    send_rows = jnp.dot(dispatch_map, normed, preferred_element_type=jnp.float32).astype(
        jnp.bfloat16
    )
    arrived = lax.all_to_all(
        send_rows.reshape(expert_count, CAP, model_width),
        "exp",
        split_axis=0,
        concat_axis=1,
        tiled=True,
    )
    local_experts = arrived.shape[0]
    portion = lax.all_gather(arrived, "ctx", axis=1, tiled=True)
    gate = jnp.einsum("end,edf->enf", portion, w_gate, preferred_element_type=jnp.float32)
    upward = jnp.einsum("end,edf->enf", portion, w_up, preferred_element_type=jnp.float32)
    activations = (jax.nn.silu(gate) * upward).astype(jnp.bfloat16)
    expert_total = lax.psum_scatter(
        jnp.einsum("enf,efd->ned", activations, w_down, preferred_element_type=jnp.float32).astype(
            jnp.bfloat16
        ),
        "ctx",
        scatter_dimension=0,
        tiled=True,
    )
    going_back = expert_total.reshape(exp_count, CAP, local_experts, model_width)
    returned = lax.all_to_all(going_back, "exp", split_axis=0, concat_axis=2, tiled=True)
    combine_map = jnp.where(slot_hot, mixing[:, :, None], 0.0)
    combine_map = jnp.transpose(combine_map, (0, 2, 1)).reshape(tok_here, CAP * expert_count)
    mixture = jnp.dot(
        combine_map,
        returned.reshape(CAP * expert_count, model_width).astype(jnp.float32),
        precision=lax.Precision.HIGHEST,
    )
    return (hidden + mixture).astype(jnp.bfloat16)


def solution(mesh):
    return jax.shard_map(
        body,
        mesh=mesh,
        in_specs=(
            P("ctx", "exp", None),
            P("ctx", "exp"),
            P(None, "ctx"),
            P(None, "ctx"),
            P(),
            P("exp", None, None),
            P("exp", "ctx"),
            P(("ctx", "exp"), None),
            P(),
            P(),
            P(("ctx", "exp"), None),
            P("exp", None, "ctx"),
            P("exp", None, "ctx"),
            P("exp", "ctx", None),
        ),
        out_specs=P(("ctx", "exp"), None),
        check_vma=False,
    )
```

profile of v0, /device:TPU:2, one launch (start us, length us, event | category | flops | bytes accessed | tf_op | source)
XLA Modules:
  0.0 589.2 jit_solution(14569055627388049429)
XLA Ops:
  6.5 1.2 copy.37
  7.7 1.6 pad_maximum_fusion
  9.4 1.0 reshape.334
  10.4 0.7 select_reduce_fusion.4
  11.1 0.8 select_reduce_fusion
  12.0 0.2 broadcast_compare_fusion
  12.2 76.2 %all-gather.3.cloned.1.call-done = bf16[576,3072]{0,1:T(8,128)(2,1)} async-done(((bf16[576,192]{0,1:T(8,128)(2,1)}), bf16[576,3072]{0,1:T(8,128)(2,1)}) %all-gather.3.cloned.1.call-update) | async-done | bytes 3538960 | tf_op jit(solution)/shard_map/all_gather | solution.py:121
  88.3 3.9 fusion.13
  92.2 3.0 fusion.90
  95.2 2.6 copy-done.1
  97.9 1.0 fusion.6
  98.9 0.1 exp.39
  99.2 5.6 fusion.37
  104.8 1.2 fusion.56
  106.1 0.3 broadcast_in_dim.120
  106.4 35.5 %all_to_all.46 = bf16[16,64,1024]{2,1,0:T(8,128)(2,1)S(1)} all-to-all(bf16[16,64,1024]{2,1,0:T(8,128)(2,1)S(1)} %broadcast_in_dim.120), channel_id=1, replica_groups=mesh['ctx'=16,'exp'=16] {'ctx'}, dimensions={0} | all-to-all | bytes 4194304 | tf_op jit(solution)/shard_map/all_to_all | solution.py:18
  141.9 1.2 copy.41
  143.0 1.4 fusion.24
  144.5 1.8 copy.43
  146.3 25.1 %all-to-all-start.1 = ((bf16[16,16,1,4,448]{4,3,1,2,0:T(4,128)(2,1)}), bf16[16,16,1,4,448]{4,3,1,2,0:T(4,128)(2,1)S(1)}, u32[]{:S(2)}, u32[]{:S(2)}) async-start(bf16[16,16,1,4,448]{4,3,1,2,0:T(4,128)(2,1)} %copy.43), calls=%async_computation.1 | async-start | bytes 2097152 | tf_op jit(solution)/shard_map/all_to_all | solution.py:40
  171.5 0.1 convert_reduce_fusion
  171.5 28.7 %all-to-all-done.1 = bf16[16,16,1,4,448]{4,3,1,2,0:T(4,128)(2,1)S(1)} async-done(((bf16[16,16,1,4,448]{4,3,1,2,0:T(4,128)(2,1)}), bf16[16,16,1,4,448]{4,3,1,2,0:T(4,128)(2,1)S(1)}, u32[]{:S(2)}, u32[]{:S(2)}) %all-to-all-start.1) | async-done | bytes 917536 | tf_op jit(solution)/shard_map/all_to_all | solution.py:40
  200.3 1.1 reduce_sum.92
  201.4 5.7 all-to-all-start.2
  207.3 0.1 and.113
  207.4 0.1 eq.95
  207.6 0.1 eq.93
  207.7 8.1 %all-to-all-done.2 = bf16[16,1,4,448]{3,2,1,0:T(4,128)(2,1)S(1)} async-done(((bf16[16,1,4,448]{3,2,1,0:T(4,128)(2,1)}), bf16[16,1,4,448]{3,2,1,0:T(4,128)(2,1)S(1)}, u32[]{:S(2)}, u32[]{:S(2)}) %all-to-all-start.2) | async-done | bytes 57376 | tf_op jit(solution)/shard_map/all_to_all | solution.py:139
  215.8 0.1 reshape.344
  216.0 0.2 multiply_reduce_fusion
  216.2 0.1 multiply_convert_fusion
  216.3 0.6 copy-done.5
  216.9 0.4 convolution_convert_fusion.1
  217.3 0.4 reshape.337
  217.8 28.8 %all_to_all.47 = bf16[16,3,7168]{2,1,0:T(4,128)(2,1)} all-to-all(bf16[16,3,7168]{2,1,0:T(4,128)(2,1)S(1)} %reshape.337), channel_id=1, replica_groups=mesh['ctx'=16,'exp'=16] {'exp'}, dimensions={0} | all-to-all | bytes 1376256 | tf_op jit(solution)/shard_map/all_to_all | solution.py:164
  246.5 2.3 all_to_all.37
  249.0 120.8 %all-gather.5.cloned.1.call-done = bf16[1,768,7168]{2,1,0:T(8,128)(2,1)} async-done(((bf16[1,48,7168]{2,1,0:T(8,128)(2,1)}), bf16[1,768,7168]{2,1,0:T(8,128)(2,1)}) %all-gather.5.cloned.1.call-update) | async-done | bytes 11010064 | tf_op jit(solution)/shard_map/all_gather | solution.py:172
  369.8 6.3 %fusion.2 = f32[768,128]{1,0:T(8,128)S(1)} fusion(bf16[1,768,7168]{2,1,0:T(8,128)(2,1)} %all-gather.5.cloned.1.call-done, bf16[1,7168,128]{2,1,0:T(8,128)(2,1)} %param.25), kind=kOutput, calls=%fused_computation.3 | convolution fusion | flops 1409286144 | bytes 13238272 | tf_op jit(solution)/shard_map/end,edf->enf/dot_general | solution.py:173
  376.1 17.3 %fusion.4 = bf16[768,1,7168]{2,0,1:T(8,128)(2,1)} fusion(bf16[1,128,7168]{2,1,0:T(8,128)(2,1)S(1)} %copy-done, bf16[1,7168,128]{2,1,0:T(8,128)(2,1)} %param.26, bf16[1,768,7168]{2,1,0:T(8,128)(2,1)} %all-gather.5.cloned.1.call-done, f32[768,128]{1,0:T(8,128)S(1)} %fusion.2), kind=kOutput, calls=%fused_computation.5 | convolution fusion | flops 2824667136 | bytes 26083328 | tf_op jit(solution)/shard_map/enf,efd->ned/dot_general | solution.py:177
  393.5 158.0 %reduce-scatter.2.cloned.1.call-done = bf16[48,1,7168]{2,0,1:T(8,128)(2,1)} async-done(((bf16[768,1,7168]{2,0,1:T(8,128)(2,1)}), bf16[48,1,7168]{2,0,1:T(8,128)(2,1)}) %reduce-scatter.2.cloned.1.call-update) | async-done | bytes 688144 | tf_op jit(solution)/shard_map/reduce_scatter | solution.py:176
  551.5 2.2 reshape.342
  553.6 4.4 all-to-all-start.4
  558.1 0.2 fusion.59
  558.3 0.2 select_reduce_fusion.1
  558.5 0.1 select_reduce_fusion.3
  558.7 22.6 %all-to-all-done.4 = bf16[16,3,1,7168]{3,1,2,0:T(4,128)(2,1)S(1)} async-done(((bf16[16,3,1,7168]{3,1,2,0:T(4,128)(2,1)}), bf16[16,3,1,7168]{3,1,2,0:T(4,128)(2,1)S(1)}, u32[]{:S(2)}, u32[]{:S(2)}) %all-to-all-start.4) | async-done | bytes 688160 | tf_op jit(solution)/shard_map/all_to_all | solution.py:185
  581.4 0.3 copy.48
  581.7 1.0 fusion.5
  (58 shorter events, 0.9 us)
Async XLA Ops:
  6.5 369.6 %copy-start = (bf16[1,128,7168]{2,1,0:T(8,128)(2,1)S(1)}, bf16[1,128,7168]{2,1,0:T(8,128)(2,1)}, u32[]{:S(2)}) copy-start(bf16[1,128,7168]{2,1,0:T(8,128)(2,1)} %param.27) | copy-start | bytes 5505028
  6.5 81.8 %all-gather.3.cloned.1.call-start = ((), (), s32[]{:S(2)}) async-start(), calls=%async_computation.6 | async-start | bytes 4177920 | tf_op jit(solution)/shard_map/all_gather | solution.py:121
  95.2 2.7 copy-start.1
  99.2 5.7 copy-start.2
  106.4 36.7 %copy-start.14 = (bf16[1024,448]{0,1:T(8,128)(2,1)S(1)}, bf16[1024,448]{0,1:T(8,128)(2,1)}, u32[]{:S(2)}) copy-start(bf16[1024,448]{0,1:T(8,128)(2,1)} %param.20) | copy-start | bytes 2752516
  144.5 27.0 %copy-start.12 = (s32[4,8]{1,0:T(4,128)S(1)}, s32[4,8]{1,0:T(4,128)}, u32[]{:S(2)}) copy-start(s32[4,8]{1,0:T(4,128)} %param.24) | copy-start | bytes 388
  144.5 71.5 %copy-start.3 = (bf16[4,7168]{1,0:T(4,128)(2,1)S(1)}, bf16[4,7168]{1,0:T(4,128)(2,1)}, u32[]{:S(2)}) copy-start(bf16[4,7168]{1,0:T(4,128)(2,1)} %param.21) | copy-start | bytes 172036
  144.5 71.7 %copy-start.9 = (f32[7168]{0:T(1024)S(1)}, f32[7168]{0:T(1024)}, u32[]{:S(2)}) copy-start(f32[7168]{0:T(1024)} %param.22) | copy-start | bytes 86020
  146.3 54.0 %all-to-all-start.1 = ((bf16[16,16,1,4,448]{4,3,1,2,0:T(4,128)(2,1)}), bf16[16,16,1,4,448]{4,3,1,2,0:T(4,128)(2,1)S(1)}, u32[]{:S(2)}, u32[]{:S(2)}) async-start(bf16[16,16,1,4,448]{4,3,1,2,0:T(4,128)(2,1)} %copy.43), calls=%async_computation.1 | async-start | bytes 2097152 | tf_op jit(solution)/shard_map/all_to_all | solution.py:40
  171.5 44.6 %copy-start.7 = (s32[4,16]{1,0:T(4,128)}, s32[4,16]{1,0:T(4,128)S(1)}, u32[]{:S(2)}) copy-start(s32[4,16]{1,0:T(4,128)S(1)} %convert_reduce_fusion) | copy-start | bytes 772
  201.4 14.4 %all-to-all-start.2 = ((bf16[16,1,4,448]{3,2,1,0:T(4,128)(2,1)}), bf16[16,1,4,448]{3,2,1,0:T(4,128)(2,1)S(1)}, u32[]{:S(2)}, u32[]{:S(2)}) async-start(bf16[16,1,4,448]{3,2,1,0:T(4,128)(2,1)} %bitcast.12), calls=%async_computation.2 | async-start | bytes 131072 | tf_op jit(solution)/shard_map/all_to_all | solution.py:139
  207.1 162.7 %all-gather.5.cloned.1.call-start = ((), (), s32[]{:S(2)}) async-start(), calls=%async_computation.7 | async-start | bytes 11698176 | tf_op jit(solution)/shard_map/all_gather | solution.py:172
  207.2 8.6 %copy-start.10 = (s32[4,16]{1,0:T(4,128)}, s32[4,16]{1,0:T(4,128)S(1)}, u32[]{:S(2)}) copy-start(s32[4,16]{1,0:T(4,128)S(1)} %sub.74) | copy-start | bytes 772
  216.3 0.6 copy-start.5
  248.9 302.5 %reduce-scatter.2.cloned.1.call-start = ((), (), s32[]{:S(2)}) async-start(), calls=%async_computation.8 | async-start | bytes 11698176 | tf_op jit(solution)/shard_map/reduce_scatter | solution.py:176
  393.4 164.6 %copy-start.8 = (s32[4,16]{1,0:T(4,128)S(1)}, s32[4,16]{1,0:T(4,128)}, u32[]{:S(2)}) copy-start(s32[4,16]{1,0:T(4,128)} %copy-done.7) | copy-start | bytes 772
  393.4 164.6 %copy-start.6 = (bf16[4,7168]{1,0:T(4,128)(2,1)S(1)}, bf16[4,7168]{1,0:T(4,128)(2,1)}, u32[]{:S(2)}) copy-start(bf16[4,7168]{1,0:T(4,128)(2,1)} %copy-done.5) | copy-start | bytes 172036
  393.4 164.7 %copy-start.15 = (bf16[7168,16]{0,1:T(8,128)(2,1)S(1)}, bf16[7168,16]{0,1:T(8,128)(2,1)}, u32[]{:S(2)}) copy-start(bf16[7168,16]{0,1:T(8,128)(2,1)} %param.23) | copy-start | bytes 688132
  393.4 164.8 %copy-start.13 = (s32[4,8]{1,0:T(4,128)S(1)}, s32[4,8]{1,0:T(4,128)}, u32[]{:S(2)}) copy-start(s32[4,8]{1,0:T(4,128)} %param.24) | copy-start | bytes 388
  393.4 165.2 %copy-start.11 = (s32[4,16]{1,0:T(4,128)S(1)}, s32[4,16]{1,0:T(4,128)}, u32[]{:S(2)}) copy-start(s32[4,16]{1,0:T(4,128)} %copy-done.10) | copy-start | bytes 772
  393.5 188.2 %copy-start.4 = (bf16[4,7168]{1,0:T(4,128)(2,1)S(1)}, bf16[4,7168]{1,0:T(4,128)(2,1)}, u32[]{:S(2)}) copy-start(bf16[4,7168]{1,0:T(4,128)(2,1)} %param.21) | copy-start | bytes 172036
  553.6 27.7 %all-to-all-start.4 = ((bf16[16,3,1,7168]{3,1,2,0:T(4,128)(2,1)}), bf16[16,3,1,7168]{3,1,2,0:T(4,128)(2,1)S(1)}, u32[]{:S(2)}, u32[]{:S(2)}) async-start(bf16[16,3,1,7168]{3,1,2,0:T(4,128)(2,1)} %bitcast.106), calls=%async_computation.5 | async-start | bytes 1835008 | tf_op jit(solution)/shard_map/all_to_all | solution.py:185
Sparse Core Ops, SparseCore 0:
  10.0 78.2 all-gather.2
  249.0 120.7 all-gather.4
  393.6 157.8 reduce-scatter.1
where the time goes:
time: 591 us; the launch traced here: 589 us
  waiting for transfers between devices  414 us (70%)
  blocking collectives  64.3 us (11%)
  matrix products  40.4 us (7%)
  starting transfers between devices  35.3 us (6%)
  local copies, waits for them, and re-layouts  14.9 us (3%)
  between operations  13.5 us (2%)
  other arithmetic  6.29 us (1%)
    reduce_scatter x1, waiting for transfers between devices, body(): lax.psum_scatter(jnp.einsum('enf,efd->ned', activations, w_down, preferre...  158 us
    all_gather x1, waiting for transfers between devices, body(): portion = lax.all_gather(arrived, 'ctx', axis=1, tiled=True)  121 us
    all_gather x1, waiting for transfers between devices, body(): portion = lax.all_gather(keys_here, 'ctx', axis=1, tiled=True)  76.2 us
    all_to_all x1, blocking collectives, copy_for_each(): return lax.all_to_all(copies, axis, split_axis=0, concat_axis=0, tiled=True)  35.5 us
    all_to_all x1, blocking collectives, body(): lax.all_to_all(send_rows.reshape(expert_count, CAP, model_width), 'exp',...  28.8 us
    all_to_all x1, waiting for transfers between devices, sum_at_owner(): lax.all_to_all(in_blocks(value, dim, length), axis, 0, 0, tiled=True)  28.7 us
    all_to_all x1, starting transfers between devices, sum_at_owner(): lax.all_to_all(in_blocks(value, dim, length), axis, 0, 0, tiled=True)  25.1 us
    all_to_all x1, waiting for transfers between devices, body(): lax.all_to_all(going_back, 'exp', split_axis=0, concat_axis=2, tiled=True)  22.6 us
  transfers between devices with their start and end apart: 6, of which 6 were waited for; matrix products, arithmetic and copies ran while one was open for 1% of the time, Pallas kernels for 0%

commit v1 on v0

v1 whole, which is shorter than its diff:
```python
import functools
import math

import jax
import jax.numpy as jnp
from jax import lax
from jax.experimental import pallas as pl
from jax.experimental.pallas import tpu as pltpu
from jax.sharding import PartitionSpec as P

QKD = 192
ROUTE_SCALE = 2.5
NORM_EPS = 1e-06
MESH = pl.DeviceIdType.MESH
BF16 = jnp.bfloat16
F32 = jnp.float32
VMEM_LIMIT = 60 * 1024 * 1024
CHUNKS = 6
ROWS = 256
LOG_SCALE = math.log2(math.e) / math.sqrt(QKD)


def coords():
    c = lax.axis_index("ctx")
    e = lax.axis_index("exp")
    core = lax.rem(c, 2)
    x = lax.rem(lax.div(c, 2), 4)
    zh = lax.div(c, 8)
    y = lax.div(e, 4)
    zl = lax.rem(e, 4)
    return core, x, y, zh, zl


def device(core, x, y, z):
    return ((lax.div(z, 4) * 4 + x) * 2 + core, y * 4 + lax.rem(z, 4))


def one(v):
    return v + 1 - 2 * lax.rem(v, 2)


def two(v):
    return lax.rem(v + 2, 4)


def three(v):
    return 3 - v


def choose(i, table):
    value = table[0]
    for n in range(1, len(table)):
        value = jnp.where(i == n, table[n], value)
    return value


def swap(core, first, second):
    return first + core * (second - first), second + core * (first - second)


class Net:
    def __init__(self, send_sems, recv_sems):
        self.send_sems, self.recv_sems = send_sems, recv_sems
        self.count = 0
        self.sent = []

    def make(self, src, dst, dev):
        index = self.count
        self.count += 1
        return pltpu.make_async_remote_copy(
            src_ref=src,
            dst_ref=dst,
            send_sem=self.send_sems.at[index],
            recv_sem=self.recv_sems.at[index],
            device_id=dev,
            device_id_type=MESH,
        )

    def plan(self, src, dst, dev):
        copy = self.make(src, dst, dev)
        self.sent.append(copy)
        return copy

    def send(self, src, dst, dev):
        copy = self.plan(src, dst, dev)
        copy.start()
        return copy

    def drain(self):
        for copy in self.sent:
            copy.wait_send()


class Later:
    def __init__(self, **kwargs):
        self.kwargs = kwargs

    def start(self):
        pltpu.make_async_remote_copy(**self.kwargs).start()

    def wait_recv(self):
        pltpu.make_async_remote_copy(**self.kwargs).wait_recv()

    def wait_send(self):
        pltpu.make_async_remote_copy(**self.kwargs).wait_send()


def greet(peers, meanwhile):
    barrier = pltpu.get_barrier_semaphore()
    for peer in peers:
        pl.semaphore_signal(barrier, inc=1, device_id=peer, device_id_type=MESH)
    meanwhile()
    pl.semaphore_wait(barrier, len(peers))


class Layer:
    def __init__(self, refs, net):
        self.__dict__.update(refs)
        self.net = net
        self.core, self.x, self.y, self.zh, self.zl = coords()
        self.z = self.zh * 4 + self.zl
        self.e = self.y * 4 + self.zl
        self.a, self.b = swap(self.core, self.y, self.x)
        core, x, y, z = self.core, self.x, self.y, self.z
        z_far = (1 - self.zh) * 4 + self.zl
        self.partner = device(1 - core, x, y, z)
        self.x_peers = [device(core, lax.rem(x + d, 4), y, z) for d in range(1, 4)]
        self.y_peers = [device(core, x, lax.rem(y + d, 4), z) for d in range(1, 4)]
        self.z_peers = [device(core, x, y, lax.rem(z + d, 8)) for d in range(1, 8)]
        self.far_peers = [device(core, lax.rem(x + d, 4), y, z_far) for d in range(4)]

    def place(self, a_, b_, z_):
        y_, x_ = swap(self.core, a_, b_)
        return device(self.core, x_, y_, z_)

    def load(self, src, dst):
        copy = pltpu.make_async_copy(src, dst, self.local_sems.at[self.loads])
        self.loads += 1
        copy.start()
        return copy

    def start(self):
        self.loads = 0
        core, x, y, zh, zl = self.core, self.x, self.y, self.zh, self.zl
        me = zh * 4 + x
        own_cache = self.load(self.cache, self.cached.at[zh, x, core])
        own_fresh = self.load(self.fresh, self.newer.at[zh, x, core])
        self.own_rows = self.load(
            self.residual.at[:, pl.ds(pl.multiple_of(me * 896, 128), 896)], self.rows_in.at[me]
        )
        self.uv_load = self.load(self.w_uv, self.uv)
        self.wo_load = self.load(
            self.w_out, self.wo.at[pl.ds(pl.multiple_of(core * 448, 64), 448)]
        )
        self.moe_loads = [
            self.load(self.w_gate, self.w_all.at[0]),
            self.load(self.w_up, self.w_all.at[1]),
            self.load(self.w_down, self.wd.at[0]),
        ]
        peers = self.x_peers + self.y_peers + self.z_peers + self.far_peers[1:] + [self.partner]
        greet(peers, self.prepare_queries)
        own_cache.wait()
        own_fresh.wait()

    def prepare_queries(self):
        x, y, zh, zl = self.x, self.y, self.zh, self.zl
        lane = lax.broadcasted_iota(jnp.int32, (1, 128), 1)
        marks = jnp.zeros((1, 128), F32)
        for j in range(4):
            for n in range(8):
                marks += jnp.where(lane == self.ids[j, n] + 16 * j, 1.0, 0.0)
        self.marks[zh, x, y, zl] = marks
        @pl.loop(0, 8)
        def _(i):
            some = pl.ds(pl.multiple_of(i * 8, 8), 8)
            rows = pl.ds(pl.multiple_of(i * 64, 64), 64)
            self.q[rows, 0:512] = self.q_nope[some].astype(F32).reshape(64, 512).astype(BF16)

        for h in range(8):
            self.pe[pl.ds(h, 64, stride=8), 0:64] = self.q_rope[:, h * 64 : h * 64 + 64].astype(F32)
        self.q[:, 512:576] = self.pe[:, 0:64].astype(BF16)
        self.peak[...] = jnp.full((512, 128), -jnp.inf, F32)
        self.mass[...] = jnp.zeros((512, 128), F32)
        self.mean[...] = jnp.zeros((4, 512, 128), F32)
    def gather_and_attend(self):
        net = self.net
        core, x, y, zh, zl, z = self.core, self.x, self.y, self.zh, self.zl, self.z
        far = 1 - zh
        x1, x2, x3 = one(x), two(x), three(x)
        to_one, to_three = device(core, x1, y, z), device(core, x3, y, z)
        parts = ((self.cached, 0, 288), (self.cached, 288, 288), (self.newer, 0, 64))

        def whole(side, column, dev):
            refs = [r.at[side, column, core, pl.ds(at, size)] for r, at, size in parts]
            return [net.plan(ref, ref, dev) for ref in refs]

        def piece(side, column, late, dev):
            refs = [
                r.at[side, column, core, pl.ds(at + late * size // 2, size // 2)] for r, at, size in parts
            ]
            return [net.plan(ref, ref, dev) for ref in refs]

        def go(copies):
            for copy in copies:
                copy.start()

        def arrive(copies):
            for copy in copies:
                copy.wait_recv()

        edge = jnp.logical_or(zl == 0, zl == 3)
        z_out = lax.rem(z + 8 + jnp.where(zl == 0, -1, 1), 8)
        z_in = lax.rem(z + 8 + jnp.where(zl == 0, 1, -1), 8)
        z_copies, z_nexts = [], []
        for r, at, size in parts:
            near_ref = r.at[zh, x, core, pl.ds(at, size)]
            far_ref = r.at[far, x, core, pl.ds(at, size)]
            z_copies.append(net.make(near_ref, near_ref, device(core, x, y, z_out)))
            z_nexts.append(net.make(far_ref, far_ref, device(core, x, y, z_in)))

        @pl.when(edge)
        def _():
            for copy in z_copies:
                copy.start()

        near = whole(zh, x, to_one), whole(zh, x, to_three)
        near_pieces = piece(zh, x1, 0, to_three), piece(zh, x3, 1, to_one)
        share = whole(far, x, to_one), whole(far, x, to_three)
        far_pieces = piece(far, x1, 0, to_three), piece(far, x3, 1, to_one)
        gifts = [whole(side, c, self.partner) for side in (zh, far) for c in (x, x1, x3, x2)]
        go(near[0] + near[1] + gifts[0])
        row_copies = []
        me = zh * 4 + x
        for d in range(7):
            column, side = lax.rem(x + (d + 1) % 4, 4), zh if d < 3 else far
            there = side * 4 + column
            row_copies.append(
                net.send(
                    self.residual.at[:, pl.ds(pl.multiple_of(there * 896, 128), 896)],
                    self.rows_in.at[me],
                    device(core, column, y, side * 4 + zl),
                )
            )
        mark = self.marks.at[zh, x, y, zl]
        marks_z = [net.send(mark, mark, p) for p in self.z_peers]
        mark = self.marks.at[:, x, y]
        marks_x = [net.plan(mark, mark, p) for p in self.x_peers]
        mark = self.marks.at[:, :, y]
        marks_y = [net.plan(mark, mark, p) for p in self.y_peers]
        wo_here = self.wo.at[pl.ds(pl.multiple_of(core * 448, 64), 448)]
        weights = [
            net.plan(self.w_out, wo_here, self.partner),
            net.plan(self.w_gate, self.w_all.at[2], self.partner),
            net.plan(self.w_up, self.w_all.at[3], self.partner),
            net.plan(self.w_down, self.wd.at[1], self.partner),
        ]

        order, first = self.order, core + 2 * me

        def pick(index, length, table):
            out = jnp.zeros(index.shape, jnp.int32)
            for n in range(length):
                out += jnp.where(index == n, order[table + n], 0)
            return out

        @pl.loop(0, 8)
        def _(i):
            @pl.when(i == 0)
            def _():
                arrive(gifts[0])

            @pl.when(i == 1)
            def _():
                for n in range(3):
                    for m in range(2):
                        near[m][n].wait_recv()
                        go([near_pieces[m][n], gifts[1 + m][n]])

                    @pl.when(edge)
                    def _():
                        z_copies[n].wait_recv()
                        z_nexts[n].start()

                arrive(gifts[1])

            @pl.when(i == 2)
            def _():
                arrive(marks_z)
                go(marks_x)
                arrive(gifts[2])

            @pl.when(i == 3)
            def _():
                for n in range(3):
                    @pl.when(jnp.logical_not(edge))
                    def _():
                        z_nexts[n].wait_recv()

                    go([share[0][n], share[1][n], gifts[4][n]])
                arrive(near_pieces[0] + near_pieces[1])
                go(gifts[3])
                arrive(gifts[3])

            @pl.when(i == 4)
            def _():
                arrive(marks_x)
                go(marks_y)
                arrive(gifts[4])

            @pl.when(i == 5)
            def _():
                for n in range(3):
                    for m in range(2):
                        share[m][n].wait_recv()
                        go([far_pieces[m][n], gifts[5 + m][n]])
                arrive(gifts[5])

            @pl.when(i == 6)
            def _():
                arrive(gifts[6])

            @pl.when(i == 7)
            def _():
                arrive(far_pieces[0] + far_pieces[1])
                go(gifts[7] + weights)
                arrive(gifts[7])

            with jax.named_scope("p_block"):
                side = jnp.where(i < 4, zh, far)
                j = lax.rem(i, 4)
                column = jnp.where(j == 0, x, jnp.where(j == 1, x1, jnp.where(j == 2, x3, x2)))
                old = jnp.concatenate([self.cached[side, column, 0], self.cached[side, column, 1]], axis=1)
                new = self.newer[side, column].reshape(128, 576)
                last = (((1,), (1,)), ((), ()))
                self.score[:, 0:256] = jnp.dot(self.q[...], old, preferred_element_type=F32)
                self.score[:, 256:384] = lax.dot_general(self.q[...], new, last, preferred_element_type=F32)
                lane = lax.broadcasted_iota(jnp.int32, (1, 128), 1)
                table = (side * 4 + column) * 4
                key_pos = pick(lax.div(lane, 32), 4, table) * 32 + lax.rem(lane, 32)

                @pl.loop(0, 512 // ROWS)
                def _(r):
                    here = pl.ds(pl.multiple_of(r * ROWS, ROWS), ROWS)
                    row = r * ROWS + lax.broadcasted_iota(jnp.int32, (ROWS, 1), 0)
                    first_pos, last_pos = order[first * 2] * 32, order[first * 2 + 1] * 32
                    pos = jnp.where(row < 256, first_pos, last_pos) + lax.rem(lax.div(row, 8), 32)
                    parts = [self.score[here, n * 128 : n * 128 + 128] * LOG_SCALE for n in range(3)]
                    parts[2] = jnp.where(key_pos <= pos, parts[2], -jnp.inf)
                    before = self.peak[here]
                    top = jnp.maximum(jnp.maximum(parts[0], parts[1]), parts[2])
                    peak = jnp.maximum(before, jnp.max(top, axis=1, keepdims=True))
                    fade = jnp.exp2(before - peak)
                    self.peak[here] = peak
                    self.fade[here] = fade
                    parts = [jnp.exp2(part - peak) for part in parts]
                    self.mass[here] = self.mass[here] * fade + (parts[0] + parts[1] + parts[2])
                    for n in range(3):
                        self.weight[here, n * 128 : n * 128 + 128] = parts[n].astype(BF16)

                added = lax.dot_general(
                    self.weight[:, 0:256], old[:512], last, preferred_element_type=F32
                ) + jnp.dot(self.weight[:, 256:384], new[:, :512], preferred_element_type=F32)
                for n in range(4):
                    self.mean[n] = self.mean[n] * self.fade[...] + added[:, n * 128 : n * 128 + 128]

        self.row_copies, self.weights, self.marks_y = row_copies, weights, marks_y
        self.edge, self.z_sent = edge, z_copies + z_nexts
        with jax.named_scope("p_values"):
            self.uv_load.wait()
            for h in range(8):
                some = pl.ds(h, 64, stride=8)
                mass = jnp.sum(self.mass[some], axis=1, keepdims=True)
                latent = jnp.concatenate([self.mean[n, some] / mass for n in range(4)], axis=1)
                high = latent.astype(BF16)
                low = (latent - high.astype(F32)).astype(BF16)
                out = jnp.dot(high, self.uv[h], preferred_element_type=F32)
                out += jnp.dot(low, self.uv[h], preferred_element_type=F32)
                self.heads[zh, x, :, h * 128 : h * 128 + 128] = out.astype(BF16)

    def prepare(self):
        for copy in [self.own_rows, self.wo_load]:
            copy.wait()
        for copy in self.row_copies + self.weights[:1] + self.marks_y:
            copy.wait_recv()
        self.rows[...] = jnp.zeros((128, 896), BF16)
        for block in range(8):
            self.rows[block * 16 : block * 16 + 4] = self.rows_in[block]

        @pl.loop(0, 128)
        def _(o):
            oy, oz = lax.div(lax.rem(o, 16), 4), lax.rem(o, 4)
            self.owners[pl.ds(o, 1)] = self.marks[lax.div(o, 64), lax.rem(lax.div(o, 16), 4), oy, oz]

        self.total[...] = jnp.zeros_like(self.total)
        self.logit[...] = jnp.zeros_like(self.logit)
        self.square[...] = jnp.zeros_like(self.square)

    def project_and_gather(self):
        net = self.net
        core, x, y, zh, zl, z, e = self.core, self.x, self.y, self.zh, self.zl, self.z, self.e
        a, b, place = self.a, self.b, self.place
        z_peers, z_far = self.z_peers, (1 - self.zh) * 4 + self.zl
        x1, x3 = one(x), three(x)
        to_one, to_three = device(core, x1, y, z), device(core, x3, y, z)

        cuts = pl.ds(0, 32), pl.ds(32, 32)
        x_sides = to_one, to_three

        def fan_out(side, half):
            ref = self.heads.at[side, x, cuts[half]]
            first = net.send(ref, ref, x_sides[half])
            second = net.send(ref, ref, x_sides[1 - half])
            return (first, second) if half == 0 else (second, first)

        def forward(side, copies):
            passed = []
            for half in range(2):
                copies[half][half].wait_recv()
                ref = self.heads.at[side, (x1, x3)[half], cuts[half]]
                passed.append(net.send(ref, ref, x_sides[1 - half]))
            return passed

        def arrive(side, copies, passed):
            copies[0][1].wait_recv()
            copies[1][0].wait_recv()
            for copy in passed:
                copy.wait_recv()

        def project(side):
            row = lax.broadcasted_iota(jnp.int32, (256, 128), 0) + side * 256
            col = lax.broadcasted_iota(jnp.int32, (256, 128), 1)
            pick = (row == lax.div(col, 16) * 64 + e * 4 + lax.rem(col, 16)) & (lax.rem(col, 16) < 4)
            pick = jnp.where(pick, 1.0, 0.0).astype(BF16)
            lhs = self.heads[side].reshape(256, 1024)
            for start, width in ((0, 256), (256, 256), (512, 256), (768, 128)):
                cols = pl.ds(start, width)
                block = lax.dot_general(
                    lhs, self.wo[cols], (((1,), (1,)), ((), ())), preferred_element_type=F32
                )
                block += jnp.dot(pick, self.rows[:, cols], preferred_element_type=F32)
                self.part[pl.ds(side * 2, 2), :, :, cols] = block.astype(BF16).reshape(2, 4, 32, width)

        with jax.named_scope("p_heads"):
            far_copies = []
            for half in range(2):
                ref = self.heads.at[zh, x, cuts[half]]
                far_copies.append(net.send(ref, ref, device(core, x, y, z_far)))
            near = fan_out(zh, 0), fan_out(zh, 1)
            self.prepare()
            near_passed = forward(zh, near)
            far = []
            for half in range(2):
                far_copies[half].wait_recv()
                far.append(fan_out(1 - zh, half))
        with jax.named_scope("p_near"):
            arrive(zh, near, near_passed)
            project(zh)
        with jax.named_scope("p_far"):
            far_passed = forward(1 - zh, far)
            arrive(1 - zh, far, far_passed)
            project(1 - zh)

        y1, y2, y3 = one(y), two(y), three(y)
        up, down = device(core, x, y1, z), device(core, x, y3, z)
        lo, hi = pl.ds(0, 2), pl.ds(2, 2)
        with jax.named_scope("p_sum_y"):
            s10 = net.send(self.part.at[y2, lo], self.y_in.at[0, 0], up)
            s20 = net.send(self.part.at[y2, hi], self.y_in.at[1, 0], down)
            s11 = net.send(self.part.at[y1, lo], self.y_in.at[0, 1], up)
            s21 = net.send(self.part.at[y3, hi], self.y_in.at[1, 1], down)
            s10.wait_recv()
            self.part[y3, lo] = (self.part[y3, lo].astype(F32) + self.y_in[0, 0].astype(F32)).astype(BF16)
            t1 = net.send(self.part.at[y3, lo], self.y_last.at[0], down)
            s20.wait_recv()
            self.part[y1, hi] = (self.part[y1, hi].astype(F32) + self.y_in[1, 0].astype(F32)).astype(BF16)
            t2 = net.send(self.part.at[y1, hi], self.y_last.at[1], up)
            s11.wait_recv()
            t1.wait_recv()
            self.part[y, lo] = (
                self.part[y, lo].astype(F32) + self.y_in[0, 1].astype(F32) + self.y_last[0].astype(F32)
            ).astype(BF16)
            s21.wait_recv()
            t2.wait_recv()
            self.part[y, hi] = (
                self.part[y, hi].astype(F32) + self.y_in[1, 1].astype(F32) + self.y_last[1].astype(F32)
            ).astype(BF16)
        with jax.named_scope("p_sum_z"):
            line = []
            for d in range(1, 4):
                there = lax.rem(zl + d, 4)
                line.append(
                    net.send(self.part.at[y, there], self.z_parts.at[d - 1], device(core, x, y, zh * 4 + there))
                )
            for copy in line:
                copy.wait_recv()
            hidden = self.part[y, zl].astype(F32)
            for d in range(3):
                hidden += self.z_parts[d].astype(F32)
            self.buf[a, b, z] = hidden[:, :768].astype(BF16)
        self.slim[z, a, b] = hidden[:, 768:].astype(BF16)

        with jax.named_scope("p_gather"):
            self.gather_rows()

    def gather_rows(self):
        net = self.net
        core, z = self.core, self.z
        a, b, place = self.a, self.b, self.place
        a1, a2, a3 = one(a), two(a), three(a)
        b1, b2, b3 = one(b), two(b), three(b)
        a_one, a_three = place(a1, b, z), place(a3, b, z)
        b_one, b_three = place(a, b1, z), place(a, b3, z)
        front, back = pl.ds(0, 4), pl.ds(4, 4)
        ref = self.buf.at[a, b, z]
        low, high = pl.ds(0, 16), pl.ds(16, 16)
        slim = self.slim
        slim_b = [net.send(slim.at[z, a, b], slim.at[z, a, b], p) for p in (b_one, b_three)]
        by_z = {d: net.send(ref, ref, self.z_peers[d - 1]) for d in (2, 6, 1, 7)}

        def fan(z_):
            ref = self.buf.at[a, b, z_]
            return [net.send(ref, ref, p) for p in (b_one, b_three, a_one, a_three)]

        def farther(d, hop, rows):
            by_z[d].wait_recv()
            z_ = lax.rem(z + 8 - d, 8)
            ref, part = self.buf.at[a, b, z_], self.buf.at[a, b, z_, rows]
            return net.send(ref, ref, self.z_peers[hop - 1]), net.send(part, part, self.z_peers[2 * hop % 8 - 1])

        with jax.named_scope("p_fan"):
            fans = [fan(z)]
            slim_b[0].wait_recv()
            ref = slim.at[z, a, b1, low]
            slim_more = [net.send(ref, ref, b_three)]
            slim_b[1].wait_recv()
            ref = slim.at[z, a, b3, high]
            slim_more.append(net.send(ref, ref, b_one))
            by_z[3], low_half = farther(2, 1, low)
            by_z[5], high_half = farther(6, 7, high)
            for d in (1, 7):
                by_z[d].wait_recv()
                fans.append(fan(lax.rem(z + 8 - d, 8)))
            for copy in slim_more:
                copy.wait_recv()
            ref = slim.at[z, a]
            slim_a = [net.send(ref, ref, p) for p in (a_one, a_three)]
            fans.append(fan(lax.rem(z + 6, 8)))
            fans.append(fan(lax.rem(z + 2, 8)))
            for d in (3, 5):
                by_z[d].wait_recv()
                fans.append(fan(lax.rem(z + 8 - d, 8)))
            low_half.wait_recv()
            high_half.wait_recv()
            fans.append(fan(lax.rem(z + 4, 8)))
            refs = slim.at[z, a1, pl.ds(0, 2)], slim.at[z, a3, pl.ds(2, 2)]
            slim_halves = [net.plan(ref, ref, dev) for ref, dev in zip(refs, (a_three, a_one))]
            slim_z = {d: net.plan(slim.at[z], slim.at[z], self.z_peers[d - 1]) for d in (2, 6, 1, 7)}
            slim_far = {}
            for d, hop, late in ((2, 1, 0), (6, 7, 2)):
                z_ = lax.rem(z + 8 - d, 8)
                part = slim.at[z_, pl.ds(late, 2)]
                slim_far[d] = (
                    net.plan(slim.at[z_], slim.at[z_], self.z_peers[hop - 1]),
                    net.plan(part, part, self.z_peers[2 * hop % 8 - 1]),
                )

        def spread(column):
            ref = self.buf.at[a, column]
            return [net.plan(ref, ref, p) for p in (a_one, a_three)]

        def halves(column):
            ref, other = self.buf.at[a1, column, front], self.buf.at[a3, column, back]
            return [net.plan(ref, ref, a_three), net.plan(other, other, a_one)]

        ref, other = self.buf.at[a, b1, front], self.buf.at[a, b3, back]
        b_halves = [net.plan(ref, ref, b_three), net.plan(other, other, b_one)]
        columns = (b, b1, b3, b2)
        spreads = [None] + [spread(column) for column in columns[1:]]
        passed = [halves(column) for column in columns]

        def go(*copies):
            for copy in copies:
                copy.start()

        def arrive(*copies):
            for copy in copies:
                copy.wait_recv()

        def pass_on(n):
            if n == 0:
                arrive(*[f[2] for f in fans])
                go(passed[0][0])
                arrive(*[f[3] for f in fans])
                go(passed[0][1])
            else:
                arrive(spreads[n][0])
                go(passed[n][0])
                arrive(spreads[n][1])
                go(passed[n][1])

        def first_sides():
            arrive(*slim_halves)
            go(*slim_z.values())
            arrive(*[f[0] for f in fans])
            go(b_halves[0], *spreads[1])
            arrive(*[f[1] for f in fans])
            go(b_halves[1], *spreads[2])

        def far_column():
            arrive(*b_halves)
            go(*spreads[3])
            for d in (2, 6):
                arrive(slim_z[d])
                go(*slim_far[d])

        def slim_products():
            arrive(slim_z[1], slim_z[7], *slim_far[2], *slim_far[6])

            @pl.loop(0, 8)
            def _(z_):
                side, row_z = lax.div(z_, 4), lax.rem(z_, 4)
                columns, weights, gains, routers = [], [], [], []
                for col_x in range(4):
                    features = pl.ds(pl.multiple_of((side * 4 + col_x) * 896 + 768, 128), 128)
                    rows = []
                    for row_y in range(4):
                        aa, bb = swap(core, row_y, col_x)
                        rows.append(slim[z_, aa, bb])
                    columns.append(jnp.concatenate(rows, axis=0))
                    weights.append(jnp.concatenate([self.w_all[n, features] for n in range(4)], axis=1))
                    gains.append(self.gain[:, features])
                    routers.append(self.router[:, features])
                piece = jnp.concatenate(columns, axis=1).astype(F32)
                square = jnp.sum(piece * piece, axis=1, keepdims=True)
                scaled = (piece * jnp.concatenate(gains, axis=1)).astype(BF16)
                total = jnp.dot(scaled, jnp.concatenate(weights, axis=0), preferred_element_type=F32)
                logit = lax.dot_general(
                    scaled, jnp.concatenate(routers, axis=1), (((1,), (1,)), ((), ())),
                    preferred_element_type=F32,
                )
                for row_y in range(4):
                    here = pl.ds(pl.multiple_of(row_y * 128 + row_z * 32, 32), 32)
                    some = slice(row_y * 32, row_y * 32 + 32)
                    self.square[here] += jnp.broadcast_to(square[some], (32, 128))
                    self.total[here] += total[some]
                    self.logit[here] += logit[some]

            arrive(*passed[1])

        def weights_here():
            for n in range(2):
                slim_a[n].wait_recv()
                slim_halves[n].start()
            for load in self.moe_loads:
                load.wait()
            for copy in self.weights[1:]:
                copy.wait_recv()

        steps = {
            0: weights_here,
            1: first_sides,
            3: lambda: pass_on(0),
            5: far_column,
            6: lambda: pass_on(1),
            8: lambda: arrive(*passed[0]),
            9: lambda: pass_on(2),
            11: slim_products,
            12: lambda: pass_on(3),
            14: lambda: arrive(*passed[2]),
            15: lambda: arrive(*passed[3]),
        }
        order_a = (a, a, a, a1, a3, a, a1, a3, a2, a1, a3, a2, a1, a3, a2, a2)
        order_b = (b, b1, b3, b, b, b2, b1, b1, b, b3, b3, b1, b2, b2, b3, b2)

        @pl.loop(0, 16)
        def _(i):
            for n, step in steps.items():
                pl.when(i == n)(step)
            with jax.named_scope("p_unit"):
                aa, bb = choose(i, order_a), choose(i, order_b)
                row_y, col_x = swap(core, aa, bb)
                here = pl.ds(pl.multiple_of(row_y * 128, 128), 128)
                for side in range(2):
                    features = pl.ds(pl.multiple_of((side * 4 + col_x) * 896, 128), 768)
                    piece = self.buf[aa, bb, pl.ds(side * 4, 4)].reshape(128, 768).astype(F32)
                    self.square[here] += jnp.broadcast_to(
                        jnp.sum(piece * piece, axis=1, keepdims=True), (128, 128)
                    )
                    scaled = (piece * self.gain[:, features]).astype(BF16)
                    weights = jnp.concatenate([self.w_all[n, features] for n in range(4)], axis=1)
                    self.total[here] += jnp.dot(scaled, weights, preferred_element_type=F32)
                    self.logit[here] += lax.dot_general(
                        scaled, self.router[:, features], (((1,), (1,)), ((), ())),
                        preferred_element_type=F32,
                    )

    def experts(self):
        core, e = self.core, self.e

        @pl.loop(0, 2)
        def _(side):
            here = pl.ds(pl.multiple_of(side * 256, 256), 256)
            scale = lax.rsqrt(self.square[here] * (1.0 / 7168.0) + NORM_EPS)
            row = lax.broadcasted_iota(jnp.int32, (256, 128), 0)
            col = lax.broadcasted_iota(jnp.int32, (256, 128), 1)
            owner = jnp.where(col == side * 64 + lax.div(row, 4), 1.0, 0.0)
            named = jnp.dot(owner, self.owners[...], preferred_element_type=F32)
            mask = jnp.zeros((256, 16), F32)
            for n in range(4):
                mask += jnp.where(lax.rem(row[:, :16], 4) == n, named[:, n * 16 : n * 16 + 16], 0.0)
            chosen = mask * jax.nn.sigmoid(self.logit[here] * scale[:, :16])
            lane = lax.broadcasted_iota(jnp.int32, (256, 16), 1)
            named = jnp.sum(jnp.where(lane == e, chosen, 0.0), axis=1, keepdims=True)
            mix = ROUTE_SCALE * named / jnp.sum(chosen, axis=1, keepdims=True)
            for i in range(2):
                gate = self.total[here, i * 256 : i * 256 + 128] * scale
                upward = self.total[here, i * 256 + 128 : i * 256 + 256] * scale
                act = (gate * jax.nn.sigmoid(gate) * upward * mix).astype(BF16)
                act = act.reshape(4, 4, 16, 128)
                for bx in range(4):
                    for by in range(4):
                        aa, bb = swap(core, by, bx)
                        self.act[aa, bb, side, :, i * 128 : i * 128 + 128] = act[bx, by]

    def own_hidden(self):
        owner = (self.zh * 4 + self.x) * 2 + lax.div(self.e, 8)
        oy, oz = lax.div(owner, 4), lax.rem(owner, 4)
        row = lax.broadcasted_iota(jnp.int32, (16, 32), 0)
        col = lax.broadcasted_iota(jnp.int32, (16, 32), 1)
        mine = jnp.where((col == lax.rem(self.e, 8) * 4 + row) & (row < 4), 1.0, 0.0).astype(BF16)
        for block in range(8):
            aa, bb = swap(self.core, oy, block % 4)
            rows = self.buf[aa, bb, block // 4 * 4 + oz]
            self.own[:, block * 896 : block * 896 + 768] = jnp.dot(
                mine, rows, preferred_element_type=F32
            )
            rows = self.slim[block // 4 * 4 + oz, aa, bb]
            self.own[:, block * 896 + 768 : block * 896 + 896] = jnp.dot(
                mine, rows, preferred_element_type=F32
            )

    def mix_down(self):
        net = self.net
        z = self.z
        a, b, place = self.a, self.b, self.place
        a1, a2, a3 = one(a), two(a), three(a)
        b1, b2, b3 = one(b), two(b), three(b)
        a_up, a_down = place(a1, b, z), place(a3, b, z)
        b_up, b_down = place(a, b1, z), place(a, b3, z)
        base, each = net.count, 19
        net.count += each * CHUNKS

        def copies(g):
            found = []

            def add(src, dst, dev):
                index = base + g * each + len(found)
                found.append(Later(
                    src_ref=src, dst_ref=dst, send_sem=net.send_sems.at[index],
                    recv_sem=net.recv_sems.at[index], device_id=dev, device_id_type=MESH,
                ))

            add(self.prod.at[0, g, a2], self.a_in.at[0, g, 0], a_up)
            add(self.prod.at[1, g, a2], self.a_in.at[1, g, 0], a_down)
            add(self.prod.at[0, g, a1], self.a_in.at[0, g, 1], a_up)
            add(self.prod.at[1, g, a3], self.a_in.at[1, g, 1], a_down)
            add(self.prod.at[0, g, a3], self.a_last.at[0, g], a_down)
            add(self.prod.at[1, g, a1], self.a_last.at[1, g], a_up)
            add(self.prod.at[0, g, a, b2], self.b_in.at[0, g, 0], b_up)
            add(self.prod.at[1, g, a, b2], self.b_in.at[1, g, 0], b_down)
            add(self.prod.at[0, g, a, b1], self.b_in.at[0, g, 1], b_up)
            add(self.prod.at[1, g, a, b3], self.b_in.at[1, g, 1], b_down)
            add(self.prod.at[0, g, a, b3], self.b_last.at[0, g], b_down)
            add(self.prod.at[1, g, a, b1], self.b_last.at[1, g], b_up)
            for d in range(1, 8):
                add(self.pack.at[g, d], self.z_in.at[g, d - 1], self.z_peers[d - 1])
            return found

        def merge(half, g, index, *sources):
            @pl.loop(0, 4)
            def _(r):
                value = self.prod[half, g, index, r].astype(F32)
                for source in sources:
                    value += source[r].astype(F32)
                self.prod[half, g, index, r] = value.astype(BF16)

        def add_in(half, g, index, *sources):
            value = self.prod[half, g, a, index].astype(F32)
            for source in sources:
                value += source[...].astype(F32)
            self.prod[half, g, a, index] = value.astype(BF16)

        def products(g):
            c = copies(g)

            @pl.loop(0, 8)
            def _(n):
                half = lax.rem(n, 2)
                index = choose(n, (a2, a2, a1, a3, a3, a1, a, a))
                cols = pl.ds(pl.multiple_of(half * 3584 + g * 512, 512), 512)
                block = jnp.dot(
                    self.act[index].reshape(128, 256), self.wd[:, :, cols].reshape(256, 512),
                    preferred_element_type=F32,
                )
                self.prod[half, g, index] = block.astype(BF16).reshape(4, 32, 512)
                for k in range(4):
                    pl.when(n == k)(c[k].start)

        def second(g):
            c = copies(g)
            c[0].wait_recv()
            merge(0, g, a3, self.a_in.at[0, g, 0])
            c[4].start()
            c[1].wait_recv()
            merge(1, g, a1, self.a_in.at[1, g, 0])
            c[5].start()

        def third(g):
            c = copies(g)
            c[2].wait_recv()
            c[4].wait_recv()
            merge(0, g, a, self.a_in.at[0, g, 1], self.a_last.at[0, g])
            c[6].start()
            c[8].start()
            c[3].wait_recv()
            c[5].wait_recv()
            merge(1, g, a, self.a_in.at[1, g, 1], self.a_last.at[1, g])
            c[7].start()
            c[9].start()

        def fourth(g):
            c = copies(g)
            c[6].wait_recv()
            add_in(0, g, b3, self.b_in.at[0, g, 0])
            c[10].start()
            c[7].wait_recv()
            add_in(1, g, b1, self.b_in.at[1, g, 0])
            c[11].start()

        def fifth(g):
            c = copies(g)
            c[8].wait_recv()
            c[10].wait_recv()
            add_in(0, g, b, self.b_in.at[0, g, 1], self.b_last.at[0, g])
            c[9].wait_recv()
            c[11].wait_recv()
            add_in(1, g, b, self.b_in.at[1, g, 1], self.b_last.at[1, g])
            value = jnp.zeros((128, 256), F32)
            for q in range(4):
                rows = self.prod[q // 2, g, a, b, :, q % 2 * 256 : q % 2 * 256 + 256]
                value += jnp.dot(self.picks[q], rows, preferred_element_type=F32)
            self.pack[g] = value.astype(BF16).reshape(8, 16, 256)
            for d in range(7):
                c[12 + d].start()

        def last(g):
            c = copies(g)
            result = self.pack[g, 0].astype(F32)
            for d in range(7):
                c[12 + d].wait_recv()
                result += self.z_in[g, d].astype(F32)
            for q in range(4):
                start = q // 2 * 3584 + q % 2 * 256 + g * 512
                cols = pl.ds(pl.multiple_of(start, 256), 256)
                self.out[:, cols] = (result[q * 4 : q * 4 + 4] + self.own[0:4, cols]).astype(BF16)
            for copy in c:
                copy.wait_send()

        v = {}
        ups = (a_up, a_down)
        b_peers = [place(a, lax.rem(b + d, 4), z) for d in range(1, 4)]
        v["z"] = [net.plan(self.v_prod.at[d], self.v_z.at[d - 1], self.z_peers[d - 1]) for d in range(1, 8)]
        v["first"] = [
            net.plan(self.v_sum.at[half, index], self.v_a.at[half, n], ups[half])
            for half, n, index in ((0, 0, a2), (1, 0, a2), (0, 1, a1), (1, 1, a3))
        ]
        v["second"] = [
            net.plan(self.v_sum.at[half, index], self.v_last.at[half], ups[1 - half])
            for half, index in ((0, a3), (1, a1))
        ]
        v["b"] = [net.plan(self.v_pack.at[d], self.v_b.at[d - 1], b_peers[d - 1]) for d in range(1, 4)]

        def v_products():
            row = lax.broadcasted_iota(jnp.int32, (256, 256), 0)
            col = lax.broadcasted_iota(jnp.int32, (256, 256), 1)
            source = lax.rem(lax.div(row, 4), 16) * 16 + lax.div(row, 64) * 4 + lax.rem(row, 4)
            order = jnp.where(col == source, 1.0, 0.0).astype(BF16)
            for side in range(2):
                rows = jnp.dot(order, self.act[:, :, side].reshape(256, 256), preferred_element_type=F32)
                self.act_z[pl.ds(side * 4, 4)] = rows.astype(BF16).reshape(4, 64, 256)

            @pl.loop(0, 8)
            def _(n):
                d = choose(n, (4, 3, 5, 2, 6, 1, 7, 0))
                for half in range(2):
                    start = half * 3584 + CHUNKS * 512
                    block = jnp.dot(
                        self.act_z[lax.rem(z + d, 8)], self.wd[:, :, start : start + 512].reshape(256, 512),
                        preferred_element_type=F32,
                    )
                    self.v_prod[d, :, half * 512 : half * 512 + 512] = block.astype(BF16)
                for k in range(1, 8):
                    pl.when(d == k)(v["z"][k - 1].start)

        def v_first():
            for copy in v["z"]:
                copy.wait_recv()
            for half in range(2):
                cols = pl.ds(half * 512, 512)
                value = self.v_prod[0, :, cols].astype(F32)
                for d in range(7):
                    value += self.v_z[d, :, cols].astype(F32)
                self.v_sum[half] = value.astype(BF16).reshape(4, 16, 512)
            for copy in v["first"]:
                copy.start()

        def v_add(half, index, *sources):
            value = self.v_sum[half, index].astype(F32)
            for source in sources:
                value += source[...].astype(F32)
            self.v_sum[half, index] = value.astype(BF16)

        def v_second():
            for half, index in ((0, a3), (1, a1)):
                v["first"][half].wait_recv()
                v_add(half, index, self.v_a.at[half, 0])
                v["second"][half].start()

        def v_third():
            for half in range(2):
                v["first"][2 + half].wait_recv()
                v["second"][half].wait_recv()
                v_add(half, a, self.v_a.at[half, 1], self.v_last.at[half])
            row = lax.broadcasted_iota(jnp.int32, (64, 16), 0)
            col = lax.broadcasted_iota(jnp.int32, (64, 16), 1)
            there = lax.rem(b + lax.div(row, 16), 4)
            value = jnp.zeros((64, 256), F32)
            for q in range(4):
                hit = (col == there * 4 + lax.rem(row, 4)) & (lax.rem(lax.div(row, 4), 4) == q)
                hit = jnp.where(hit, 1.0, 0.0).astype(BF16)
                rows = self.v_sum[q // 2, a, :, q % 2 * 256 : q % 2 * 256 + 256]
                value += jnp.dot(hit, rows, preferred_element_type=F32)
            self.v_pack[...] = value.astype(BF16).reshape(4, 16, 256)
            for copy in v["b"]:
                copy.start()

        def v_finish():
            result = self.v_pack[0].astype(F32)
            for d in range(3):
                v["b"][d].wait_recv()
                result += self.v_b[d].astype(F32)
            for q in range(4):
                start = q // 2 * 3584 + q % 2 * 256 + CHUNKS * 512
                cols = slice(start, start + 256)
                self.out[:, cols] = (result[q * 4 : q * 4 + 4] + self.own[0:4, cols]).astype(BF16)

        row = lax.broadcasted_iota(jnp.int32, (128, 32), 0)
        col = lax.broadcasted_iota(jnp.int32, (128, 32), 1)
        there = lax.rem(z + lax.div(row, 16), 8)
        for q in range(4):
            hit = (col == there * 4 + lax.rem(row, 4)) & (lax.rem(lax.div(row, 4), 4) == q)
            self.picks[q] = jnp.where(hit, 1.0, 0.0).astype(BF16)
        stages = (products, second, third, fourth, fifth, last)

        @pl.loop(0, CHUNKS + len(stages) - 1)
        def _(t):
            for n, stage in enumerate(stages):
                g = t - n

                @pl.when((g >= 0) & (g < CHUNKS))
                def _():
                    with jax.named_scope("p_stage%d" % n):
                        stage(g)

            @pl.when(t == 1)
            def _():
                with jax.named_scope("p_v0"):
                    v_products()
                self.own_hidden()

            for n, stage in enumerate((v_first, v_second, v_third, v_finish)):
                @pl.when(t == 7 + n)
                def _():
                    with jax.named_scope("p_v%d" % (n + 1)):
                        stage()

    def finish(self):
        @pl.when(self.edge)
        def _():
            for copy in self.z_sent:
                copy.wait_send()

        self.net.drain()


ANY = pl.BlockSpec(memory_space=pl.ANY)
VM = pl.BlockSpec(memory_space=pltpu.VMEM)
SM = pl.BlockSpec(memory_space=pltpu.SMEM)
DMA = pltpu.SemaphoreType.DMA
INPUTS = (
    ("q_nope", VM), ("q_rope", VM), ("cache", ANY), ("fresh", ANY), ("order", SM), ("w_uv", ANY),
    ("w_out", ANY), ("residual", ANY), ("gain", VM), ("router", VM), ("ids", SM), ("w_gate", ANY),
    ("w_up", ANY), ("w_down", ANY),
)
SCRATCH = (
    ("cached", (2, 4, 2, 576, 128), BF16),
    ("newer", (2, 4, 2, 64, 576), BF16),
    ("rows_in", (8, 4, 896), BF16),
    ("rows", (128, 896), BF16),
    ("marks", (2, 4, 4, 4, 1, 128), F32),
    ("owners", (128, 128), F32),
    ("uv", (8, 512, 128), BF16),
    ("wo", (896, 1024), BF16),
    ("w_all", (4, 7168, 128), BF16),
    ("wd", (2, 128, 7168), BF16),
    ("q", (512, 576), BF16),
    ("pe", (512, 128), F32),
    ("score", (512, 384), F32),
    ("weight", (512, 384), BF16),
    ("peak", (512, 128), F32),
    ("mass", (512, 128), F32),
    ("mean", (4, 512, 128), F32),
    ("fade", (512, 128), F32),
    ("heads", (2, 4, 64, 1024), BF16),
    ("part", (4, 4, 32, 896), BF16),
    ("y_in", (2, 2, 2, 32, 896), BF16),
    ("y_last", (2, 2, 32, 896), BF16),
    ("z_parts", (3, 32, 896), BF16),
    ("buf", (4, 4, 8, 32, 768), BF16),
    ("slim", (8, 4, 4, 32, 128), BF16),
    ("total", (512, 512), F32),
    ("logit", (512, 16), F32),
    ("square", (512, 128), F32),
    ("act", (4, 4, 2, 16, 256), BF16),
    ("own", (16, 7168), F32),
    ("prod", (2, CHUNKS, 4, 4, 32, 512), BF16),
    ("a_in", (2, CHUNKS, 2, 4, 32, 512), BF16),
    ("a_last", (2, CHUNKS, 4, 32, 512), BF16),
    ("b_in", (2, CHUNKS, 2, 32, 512), BF16),
    ("b_last", (2, CHUNKS, 32, 512), BF16),
    ("act_z", (8, 64, 256), BF16),
    ("v_prod", (8, 64, 1024), BF16),
    ("v_z", (7, 64, 1024), BF16),
    ("v_sum", (2, 4, 16, 512), BF16),
    ("v_a", (2, 2, 16, 512), BF16),
    ("v_last", (2, 16, 512), BF16),
    ("v_pack", (4, 16, 256), BF16),
    ("v_b", (3, 16, 256), BF16),
    ("picks", (4, 128, 32), BF16),
    ("pack", (CHUNKS, 8, 16, 256), BF16),
    ("z_in", (CHUNKS, 7, 16, 256), BF16),
)
COPIES = 400


def layer_kernel(*refs):
    names = [n for n, _ in INPUTS] + ["out"] + [n for n, *_ in SCRATCH]
    layer = Layer(dict(zip(names, refs)), Net(*refs[-2:]))
    layer.local_sems = refs[-3]
    with jax.named_scope("p_start"):
        layer.start()
    with jax.named_scope("p_attend"):
        layer.gather_and_attend()
    with jax.named_scope("p_project"):
        layer.project_and_gather()
    with jax.named_scope("p_experts"):
        layer.experts()
    with jax.named_scope("p_down"):
        layer.mix_down()
    layer.finish()


def body(
    q_nope, q_rope, cache_keys, fresh_keys, block_order, w_uv, w_out, residual,
    norm_gain, router_weight, expert_ids, w_gate, w_up, w_down,
):
    return pl.pallas_call(
        layer_kernel,
        out_shape=jax.ShapeDtypeStruct((4, 7168), BF16),
        in_specs=[spec for _, spec in INPUTS],
        out_specs=VM,
        scratch_shapes=[pltpu.VMEM(dims, kind) for _, dims, kind in SCRATCH]
        + [DMA((8,)), DMA((COPIES,)), DMA((COPIES,))],
        compiler_params=pltpu.CompilerParams(
            collective_id=0, has_side_effects=True, vmem_limit_bytes=VMEM_LIMIT
        ),
    )(
        q_nope, q_rope, cache_keys, fresh_keys.T, block_order, w_uv, w_out.T, residual,
        norm_gain.reshape(1, 7168), router_weight.T, expert_ids, w_gate[0], w_up[0], w_down[0],
    )


def solution(mesh):
    return jax.shard_map(
        body,
        mesh=mesh,
        in_specs=(
            P("ctx", "exp", None),
            P("ctx", "exp"),
            P(None, "ctx"),
            P(None, "ctx"),
            P(),
            P("exp", None, None),
            P("exp", "ctx"),
            P(("ctx", "exp"), None),
            P(),
            P(),
            P(("ctx", "exp"), None),
            P("exp", None, "ctx"),
            P("exp", None, "ctx"),
            P("exp", "ctx", None),
        ),
        out_specs=P(("ctx", "exp"), None),
        check_vma=False,
    )
```

time: 591 us -> 172 us (0.29)
  waiting for transfers between devices: 414 us -> 0 us
  Pallas kernels: 0 us -> 171 us
  blocking collectives: 64.3 us -> 0 us
  matrix products: 40.4 us -> 0 us
  starting transfers between devices: 35.3 us -> 0 us
  between operations: 13.5 us -> 0.01 us
  local copies, waits for them, and re-layouts: 14.9 us -> 1.46 us
  other arithmetic: 6.29 us -> 0 us
    all_gather x2 -> x0, waiting for transfers between devices: 197 us -> none  [the longest x1 121 us: body(): portion = lax.all_gather(arrived, 'ctx', axis=1, tiled=True)]
    pallas_call x0 -> x1, Pallas kernels: none -> 171 us  [body(): pl.pallas_call(layer_kernel, out_shape=jax.ShapeDtypeStruct((4, 7168), BF...]
    reduce_scatter x1 -> x0, waiting for transfers between devices: 158 us -> none  [body(): lax.psum_scatter(jnp.einsum('enf,efd->ned', activations, w_down, preferre...]
    all_to_all x2 -> x0, blocking collectives: 64.3 us -> none  [the longest x1 35.5 us: copy_for_each(): return lax.all_to_all(copies, axis, split_axis=0, concat_axis=0, tiled=True)]
    all_to_all x3 -> x0, waiting for transfers between devices: 59.5 us -> none  [the longest x1 28.7 us: sum_at_owner(): lax.all_to_all(in_blocks(value, dim, length), axis, 0, 0, tiled=True)]
    dot_general x10 -> x0, matrix products: 40.4 us -> none  [the longest x1 17.3 us: body(): jnp.einsum('enf,efd->ned', activations, w_down, preferred_element_type=jn...]
    all_to_all x3 -> x0, starting transfers between devices: 35.2 us -> none  [the longest x1 25.1 us: sum_at_owner(): lax.all_to_all(in_blocks(value, dim, length), axis, 0, 0, tiled=True)]
  transfers between devices with their start and end apart: 6 -> 0, of which waited for: 6 -> 0; matrix products, arithmetic and copies ran while one was open for 1% -> 0% of each run, Pallas kernels for 0% -> 0%
where the time goes in v1:
time: 172 us
  Pallas kernels  171 us (99%)
    pallas_call x1, Pallas kernels, body(): pl.pallas_call(layer_kernel, out_shape=jax.ShapeDtypeStruct((4, 7168), BF...  171 us

profile of v1, /device:TPU:2, one launch (start us, length us, event | category | flops | bytes accessed | tf_op | source)
XLA Modules:
  0.0 172.0 jit_solution(1163467979792000556)
XLA Ops:
  0.0 170.5 %shard_map.136 = bf16[4,7168]{1,0:T(4,128)(2,1)} custom-call(bf16[64,8,512]{2,1,0:T(8,128)(2,1)} %refs_0_.1, bf16[64,512]{1,0:T(8,128)(2,1)} %refs_1_.1, bf16[576,128]{1,0:T(8,128)(2,1)} %refs_2_.1, bf16[64,576]{1,0:T(8,128)(2,1)} %bitcast.12, s32[32]{0:T(128)} %refs_4_.1, bf16[8,512,128]{2,1,0:T(8,128)(2,1)} %refs_5_.1, bf16[448,1024]{1,0:T(8,128)(2,1)} %bitcast.10, ...), custom_call_target="tpu_custom_call" | custom-call | tf_op jit(solution)/shard_map/pallas_call | solution.py:1077
  170.5 1.5 copy.16

commit v2 on v1

--- a/solution.py
+++ b/solution.py
@@ -962,10 +962,10 @@
             self.picks[q] = jnp.where(hit, 1.0, 0.0).astype(BF16)
         stages = (products, second, third, fourth, fifth, last)
 
-        @pl.loop(0, CHUNKS + len(stages) - 1)
+        @pl.loop(0, CHUNKS + len(stages) + 1)
         def _(t):
             for n, stage in enumerate(stages):
-                g = t - n
+                g = t - n - 2 * (n // 5)
 
                 @pl.when((g >= 0) & (g < CHUNKS))
                 def _():
@@ -979,7 +979,7 @@
                 self.own_hidden()
 
             for n, stage in enumerate((v_first, v_second, v_third, v_finish)):
-                @pl.when(t == 7 + n)
+                @pl.when(t == 6 + n)
                 def _():
                     with jax.named_scope("p_v%d" % (n + 1)):
                         stage()

time: 172 us -> 170 us (0.988)
  Pallas kernels: 171 us -> 168 us
    pallas_call x1, Pallas kernels: 171 us -> 168 us  [body(): pl.pallas_call(layer_kernel, out_shape=jax.ShapeDtypeStruct((4, 7168), BF...]
where the time goes in v2:
time: 170 us; the launch traced here: 169 us
  Pallas kernels  168 us (99%)
    pallas_call x1, Pallas kernels, body(): pl.pallas_call(layer_kernel, out_shape=jax.ShapeDtypeStruct((4, 7168), BF...  168 us

profile of v2, /device:TPU:2, one launch (start us, length us, event | category | flops | bytes accessed | tf_op | source)
XLA Modules:
  0.0 169.4 jit_solution(13872912398506458661)
XLA Ops:
  0.0 167.9 %shard_map.136 = bf16[4,7168]{1,0:T(4,128)(2,1)} custom-call(bf16[64,8,512]{2,1,0:T(8,128)(2,1)} %refs_0_.1, bf16[64,512]{1,0:T(8,128)(2,1)} %refs_1_.1, bf16[576,128]{1,0:T(8,128)(2,1)} %refs_2_.1, bf16[64,576]{1,0:T(8,128)(2,1)} %bitcast.12, s32[32]{0:T(128)} %refs_4_.1, bf16[8,512,128]{2,1,0:T(8,128)(2,1)} %refs_5_.1, bf16[448,1024]{1,0:T(8,128)(2,1)} %bitcast.10, ...), custom_call_target="tpu_custom_call" | custom-call | tf_op jit(solution)/shard_map/pallas_call | solution.py:1077
  168.0 1.5 copy.16
